TPU v7x, 32 devices: a whole 2x2x4 slice. The times are simulated.
32 devices in a mesh: rep: 1, dp: 32 (over x, y, z, core).
Axes of the slice: x: 2, y: 2, z: 4, core: 2. Of those that a mesh axis runs over, the one named last changes fastest.
Arguments:
- a: bfloat16 [32, 2, 4096, 1024], P(('rep', 'dp'))
- g: bfloat16 [32, 2, 4096, 4096], P(('rep', 'dp'))
Outputs:
- output: bfloat16 [2, 1024, 4096], P('rep')
All inputs are finite; a program needn't handle non-finite values.
Results may differ from a plain program's by a relative error of at most 0.012.
Values are sent between devices in bfloat16 or wider.
A program may use at most 2 GiB of HBM per device.

v0:
```python
import jax
import jax.numpy as jnp


def solution(mesh):
    groups = mesh.shape["rep"]

    def step(a, g):
        a, g = (t.reshape(groups, -1, *t.shape[1:]) for t in (a, g))
        sums = jnp.einsum("rsntd,rsntf->rndf", a, g, preferred_element_type=jnp.float32)
        return sums.astype(jnp.bfloat16).reshape(-1, *sums.shape[2:])

    return step
```

profile of v0, /device:TPU:0, one launch (start us, length us, event | category | flops | bytes accessed | tf_op | source)
XLA Modules:
  0.0 626.0 jit_solution(13708129825211286615)
XLA Ops:
  0.0 79.3 %fusion = f32[2,1024,4096]{2,1,0:T(8,128)} fusion(bf16[1,2,4096,4096]{3,2,1,0:T(8,128)(2,1)} %param.1, bf16[1,2,4096,1024]{3,2,1,0:T(8,128)(2,1)} %param), kind=kOutput, calls=%fused_computation | convolution fusion | flops 68719476736 | bytes 117440512 | tf_op jit(solution)/rsntd,rsntf->rndf/dot_general | solution.py:10
  79.3 546.8 %all-reduce.2 = bf16[2,1024,4096]{2,1,0:T(8,128)(2,1)} all-reduce(f32[2,1024,4096]{2,1,0:T(8,128)} %fusion), channel_id=1, replica_groups=mesh['axis_0'=32] {'axis_0'}, use_global_device_ids=true, to_apply=%add.clone | all-reduce | flops 8388608 | bytes 50331648 | tf_op jit(solution)/rsntd,rsntf->rndf/dot_general | solution.py:10
where the time goes:
time: 626 us
  blocking collectives  547 us (87%)
  matrix products  79.3 us (13%)
    dot_general x1, blocking collectives, step(): jnp.einsum('rsntd,rsntf->rndf', a, g, preferred_element_type=jnp.float32)  547 us
    dot_general x1, matrix products, step(): jnp.einsum('rsntd,rsntf->rndf', a, g, preferred_element_type=jnp.float32)  79.3 us

commit v1 on v0

v1 whole, which is shorter than its diff:
```python
import jax
import jax.numpy as jnp
from jax import lax
from jax.experimental import pallas as pl
from jax.experimental.pallas import tpu as pltpu
from jax.sharding import PartitionSpec as P

MESH = pl.DeviceIdType.MESH
TOKENS, D, FF, MATS = 4096, 1024, 4096, 2
COLS = 512
PER = FF // COLS
UNITS = MATS * PER
ROWS = (512, 256, 128, 64, 32)
LEVELS = 5
SEND_SLOTS = 4

REDUCE = ((1, 1, 0), (2, 2, 1), (3, 3, 2), (4, 4, 1), (5, 5, 1))
GATHER = ((6, 7, 3), (7, 8, 3), (8, 9, 3), (9, 10, 3))


TAIL = (
    (1, 15), (10, 0), (6, 5), (6, 6), (10, 1), (6, 7), (6, 8), (10, 2), (6, 9), (2, 14), (4, 12), (3, 13),
    (7, 4), (5, 11), (6, 10), (9, 3), (3, 14), (10, 3), (2, 15), (5, 12), (7, 5), (7, 6), (8, 4), (7, 7),
    (7, 8), (7, 9), (6, 11), (4, 13), (7, 10), (3, 15), (4, 14), (6, 12), (9, 4), (8, 5), (7, 11), (10, 4),
    (7, 12), (8, 6), (9, 5), (8, 7), (10, 5), (9, 6), (8, 8), (10, 6), (9, 7), (8, 9), (10, 7), (5, 13),
    (4, 15), (9, 8), (8, 10), (10, 8), (5, 14), (9, 9), (10, 9), (8, 11), (9, 10), (8, 12), (10, 10), (6, 13),
    (5, 15), (9, 11), (6, 14), (10, 11), (9, 12), (7, 13), (6, 15), (7, 14), (10, 12), (7, 15), (8, 13), (8, 14),
    (9, 13), (8, 15), (10, 13), (9, 14), (10, 14), (9, 15), (10, 15),
)


def kernel(a_ref, g_ref, o_ref, a_v, g_v, p_v, k1, k2, k3, k4, s0, s1, s2, s3, s4, r0, r1, r2, r3, r4,
           a_sem, g_sem, send_sem, recv_sem):
    me = lax.axis_index("dp")
    x, y, z, c = me // 16, (me // 8) % 2, (me // 2) % 4, me % 2
    zl, zh = z % 2, z // 2

    def at(x, y, z, c):
        return ((x * 2 + y) * 4 + z) * 2 + c

    first = at(x * c + (1 - x) * (1 - c), y * (1 - c) + (1 - y) * c, z, c)
    second = at(x * (1 - c) + (1 - x) * c, y * c + (1 - y) * (1 - c), z, c)
    partner = (at(x, y, z, 1 - c), first, at(x, y, z + 1 - 2 * zl, c), second, at(x, y, z + 2 - 4 * zh, c))
    bit = (c, x * (1 - c) + y * c, zl, y * (1 - c) + x * c, zh)
    base = [0]
    for lvl in range(LEVELS):
        base.append(base[-1] + bit[lvl] * ROWS[lvl])

    stage = (s0, s1, s2, s3, s4)
    recv = (r0, r1, r2, r3, r4)
    keep = (None, k1, k2, k3, k4)

    def remote(src, dst, lvl, s, u):
        return pltpu.make_async_remote_copy(
            src, dst, send_sem.at[s, u % SEND_SLOTS], recv_sem.at[s, u],
            device_id=(0, partner[lvl]), device_id_type=MESH)

    def reduce_copy(lvl, u):
        return remote(stage[lvl].at[u % 2], recv[lvl].at[u], lvl, lvl, u)

    def out_at(u, row, rows):
        col = pl.multiple_of((u % PER) * COLS, COLS)
        return (u // PER, pl.ds(pl.multiple_of(row, 32), rows), pl.ds(col, COLS))

    def gather_copy(lvl, u):
        where = o_ref.at[out_at(u, base[lvl + 1], ROWS[lvl])]
        return remote(where, where, lvl, 9 - lvl, u)

    def when(cond, fn):
        if cond is True:
            fn()
        elif cond is not False:
            pl.when(cond)(fn)

    def reduce_stage(lvl, u):
        reduce_copy(lvl - 1, u).wait_recv()
        got, rows = recv[lvl - 1].at[u], ROWS[lvl - 1]
        half = rows // 2
        if lvl < LEVELS:
            when(u >= 2, lambda: reduce_copy(lvl, u - 2).wait_send())
            go = pl.multiple_of((1 - bit[lvl]) * half, half)
            st = pl.multiple_of(bit[lvl] * half, half)
            if lvl == 1:
                out, mine = p_v[u % 2, 0], p_v[u % 2, 1]
            else:
                held = keep[lvl - 1].at[u % 2]
                out, mine = held[pl.ds(go, half)], held[pl.ds(st, half)]
            stage[lvl][u % 2] = (out + got[pl.ds(go, half)].astype(jnp.float32)).astype(jnp.bfloat16)
            keep[lvl][u % 2] = mine + got[pl.ds(st, half)].astype(jnp.float32)
            reduce_copy(lvl, u).start()
        else:
            total = keep[lvl - 1][u % 2] + got[...].astype(jnp.float32)
            o_ref[out_at(u, base[LEVELS], rows)] = total.astype(jnp.bfloat16)
            when(u >= SEND_SLOTS, lambda: gather_copy(LEVELS - 1, u - SEND_SLOTS).wait_send())
            gather_copy(LEVELS - 1, u).start()

    def gather_stage(s, u):
        lvl = 10 - s
        gather_copy(lvl, u).wait_recv()
        if lvl > 0:
            when(u >= SEND_SLOTS, lambda: gather_copy(lvl - 1, u - SEND_SLOTS).wait_send())
            gather_copy(lvl - 1, u).start()

    def run(s, u):
        reduce_stage(s, u) if s <= LEVELS else gather_stage(s, u)

    def a_copy(m, d):
        col = pl.multiple_of(d * 256, 256)
        return pltpu.make_async_copy(a_ref.at[0, m, :, pl.ds(col, 256)], a_v.at[d], a_sem.at[d])

    def g_copy(u):
        col = pl.multiple_of((u % PER) * COLS, COLS)
        return pltpu.make_async_copy(g_ref.at[0, u // PER, :, pl.ds(col, COLS)], g_v.at[u % 2], g_sem.at[u % 2])

    block = (2 * (1 - c), 2 * (1 - c) + 1, 2 * c + 1 - bit[1], 2 * c + bit[1])

    a_copy(0, block[0]).start()
    g_copy(0).start()
    for j in range(1, 4):
        a_copy(0, block[j]).start()

    barrier = pltpu.get_barrier_semaphore()
    for p in partner:
        pl.semaphore_signal(barrier, inc=1, device_id=(0, p), device_id_type=MESH)
    pl.semaphore_wait(barrier, LEVELS)

    @pl.loop(0, UNITS)
    def _(t):
        pl.when(t + 1 < UNITS)(lambda: g_copy(t + 1).start())
        g_copy(t).wait()
        m = t // PER
        for j in range(4):
            pl.when(t % PER == 0)(lambda: a_copy(m, block[j]).wait())
            if j == 0:
                pl.when(t >= 2)(lambda: reduce_copy(0, t - 2).wait_send())
            r = lax.dot_general(a_v[block[j]], g_v[t % 2], (((0,), (0,)), ((), ())),
                                preferred_element_type=jnp.float32)
            if j < 2:
                s0[t % 2, j * 256:(j + 1) * 256] = r.astype(jnp.bfloat16)
            else:
                p_v[t % 2, j - 2] = r
            pl.when(t == PER - 1)(lambda: a_copy(1, block[j]).start())
            if j == 1:
                reduce_copy(0, t).start()
            for s, lag, gap in REDUCE:
                if gap == j:
                    pl.when(t >= lag)(lambda: run(s, t - lag))
            for s, off, gap in GATHER:
                if gap == j:
                    pl.when((t >= off) & ((t - off) % 2 == 0))(lambda: run(s, (t - off) // 2))

    for s, u in TAIL:
        run(s, u)
    for lvl in range(LEVELS):
        for u in range(UNITS - 2, UNITS):
            reduce_copy(lvl, u).wait_send()
        for u in range(UNITS - SEND_SLOTS, UNITS):
            gather_copy(lvl, u).wait_send()


def solution(mesh):
    def body(a, g):
        f32, bf16 = jnp.float32, jnp.bfloat16
        return pl.pallas_call(
            kernel,
            out_shape=pltpu.VMEM((MATS, D, FF), bf16),
            in_specs=[pl.BlockSpec(memory_space=pl.ANY)] * 2,
            out_specs=pl.BlockSpec(memory_space=pltpu.VMEM),
            scratch_shapes=[
                pltpu.VMEM((4, TOKENS, 256), bf16),
                pltpu.VMEM((2, TOKENS, COLS), bf16),
                pltpu.VMEM((2, 2, 256, COLS), f32),
                *(pltpu.VMEM((2, rows, COLS), f32) for rows in ROWS[1:]),
                *(pltpu.VMEM((2, rows, COLS), bf16) for rows in ROWS),
                *(pltpu.VMEM((UNITS, rows, COLS), bf16) for rows in ROWS),
                pltpu.SemaphoreType.DMA((4,)),
                pltpu.SemaphoreType.DMA((2,)),
                pltpu.SemaphoreType.DMA((10, SEND_SLOTS)),
                pltpu.SemaphoreType.DMA((10, UNITS)),
            ],
            compiler_params=pltpu.CompilerParams(
                collective_id=0, has_side_effects=True, vmem_limit_bytes=47 * 2**20),
            cost_estimate=pl.CostEstimate(flops=2 * MATS * TOKENS * D * FF, bytes_accessed=84 * 2**20, transcendentals=0),
            name="sum_units",
        )(a, g)

    every = P(("rep", "dp"))
    return jax.shard_map(body, mesh=mesh, in_specs=(every, every), out_specs=P("rep"), check_vma=False)
```

time: 626 us -> 178 us (0.28)
  blocking collectives: 547 us -> 0 us
  Pallas kernels: 0 us -> 171 us
  matrix products: 79.3 us -> 0 us
    dot_general x1 -> x0, blocking collectives: 547 us -> none  [step(): jnp.einsum('rsntd,rsntf->rndf', a, g, preferred_element_type=jnp.float32)]
    pallas_call x0 -> x1, Pallas kernels: none -> 171 us  [body(): pl.pallas_call(kernel, out_shape=pltpu.VMEM((MATS, D, FF), bf16), in_spec...]
    dot_general x1 -> x0, matrix products: 79.3 us -> none  [step(): jnp.einsum('rsntd,rsntf->rndf', a, g, preferred_element_type=jnp.float32)]
where the time goes in v1:
time: 178 us; the launch traced here: 177 us
  Pallas kernels  171 us (96%)
  local copies, waits for them, and re-layouts  6.16 us (3%)
    pallas_call x1, Pallas kernels, body(): pl.pallas_call(kernel, out_shape=pltpu.VMEM((MATS, D, FF), bf16), in_spec...  171 us
    unnamed x1, local copies, waits for them, and re-layouts  6.16 us

profile of v1, /device:TPU:0, one launch (start us, length us, event | category | flops | bytes accessed | tf_op | source)
XLA Modules:
  0.0 177.3 jit_solution(2444607004662489144)
XLA Ops:
  0.0 171.1 %sum_units.1 = bf16[2,1024,4096]{2,1,0:T(8,128)(2,1)S(1)} custom-call(bf16[1,2,4096,1024]{3,2,1,0:T(8,128)(2,1)} %a_ref.1, bf16[1,2,4096,4096]{3,2,1,0:T(8,128)(2,1)} %g_ref.1), custom_call_target="tpu_custom_call" | custom-call | flops 68719476736 | bytes 88080384 | tf_op jit(solution)/shard_map/sum_units/pallas_call | solution.py:164
  171.1 6.2 %copy.4 = bf16[2,1024,4096]{2,1,0:T(8,128)(2,1)} copy(bf16[2,1024,4096]{2,1,0:T(8,128)(2,1)S(1)} %sum_units.1) | data formatting | bytes 33554432

commit v2 on v1

--- a/solution.py
+++ b/solution.py
@@ -12,20 +12,18 @@
 UNITS = MATS * PER
 ROWS = (512, 256, 128, 64, 32)
 LEVELS = 5
-SEND_SLOTS = 4
+STAGE_SLOTS = 2
+SEND_SLOTS = 8
 
-REDUCE = ((1, 1, 0), (2, 2, 1), (3, 3, 2), (4, 4, 1), (5, 5, 1))
-GATHER = ((6, 7, 3), (7, 8, 3), (8, 9, 3), (9, 10, 3))
-
-
+REDUCE = (3, 7, 13, 16, 22)
+GATHER, RATE = (25, 29, 40, 51), 5
 TAIL = (
-    (1, 15), (10, 0), (6, 5), (6, 6), (10, 1), (6, 7), (6, 8), (10, 2), (6, 9), (2, 14), (4, 12), (3, 13),
-    (7, 4), (5, 11), (6, 10), (9, 3), (3, 14), (10, 3), (2, 15), (5, 12), (7, 5), (7, 6), (8, 4), (7, 7),
-    (7, 8), (7, 9), (6, 11), (4, 13), (7, 10), (3, 15), (4, 14), (6, 12), (9, 4), (8, 5), (7, 11), (10, 4),
-    (7, 12), (8, 6), (9, 5), (8, 7), (10, 5), (9, 6), (8, 8), (10, 6), (9, 7), (8, 9), (10, 7), (5, 13),
-    (4, 15), (9, 8), (8, 10), (10, 8), (5, 14), (9, 9), (10, 9), (8, 11), (9, 10), (8, 12), (10, 10), (6, 13),
-    (5, 15), (9, 11), (6, 14), (10, 11), (9, 12), (7, 13), (6, 15), (7, 14), (10, 12), (7, 15), (8, 13), (8, 14),
-    (9, 13), (8, 15), (10, 13), (9, 14), (10, 14), (9, 15), (10, 15),
+    (3, 13), (10, 0), (6, 8), (10, 1), (8, 5), (9, 3), (6, 9), (7, 7), (10, 2), (9, 4), (10, 3), (8, 6),
+    (4, 12), (10, 4), (5, 11), (6, 10), (2, 15), (4, 13), (3, 14), (7, 8), (8, 7), (9, 5), (7, 9), (5, 12),
+    (10, 5), (6, 11), (9, 6), (3, 15), (7, 10), (4, 14), (10, 6), (5, 13), (8, 8), (9, 7), (7, 11), (4, 15),
+    (10, 7), (8, 9), (6, 12), (9, 8), (8, 10), (10, 8), (5, 14), (9, 9), (6, 13), (7, 12), (10, 9), (8, 11),
+    (9, 10), (5, 15), (7, 13), (6, 14), (10, 10), (8, 12), (9, 11), (6, 15), (7, 14), (10, 11), (8, 13), (9, 12),
+    (7, 15), (8, 14), (10, 12), (9, 13), (10, 13), (8, 15), (9, 14), (10, 14), (9, 15), (10, 15),
 )
 
 
@@ -56,7 +54,7 @@
             device_id=(0, partner[lvl]), device_id_type=MESH)
 
     def reduce_copy(lvl, u):
-        return remote(stage[lvl].at[u % 2], recv[lvl].at[u], lvl, lvl, u)
+        return remote(stage[lvl].at[u % STAGE_SLOTS], recv[lvl].at[u], lvl, lvl, u)
 
     def out_at(u, row, rows):
         col = pl.multiple_of((u % PER) * COLS, COLS)
@@ -77,7 +75,7 @@
         got, rows = recv[lvl - 1].at[u], ROWS[lvl - 1]
         half = rows // 2
         if lvl < LEVELS:
-            when(u >= 2, lambda: reduce_copy(lvl, u - 2).wait_send())
+            when(u >= STAGE_SLOTS, lambda: reduce_copy(lvl, u - STAGE_SLOTS).wait_send())
             go = pl.multiple_of((1 - bit[lvl]) * half, half)
             st = pl.multiple_of(bit[lvl] * half, half)
             if lvl == 1:
@@ -85,7 +83,7 @@
             else:
                 held = keep[lvl - 1].at[u % 2]
                 out, mine = held[pl.ds(go, half)], held[pl.ds(st, half)]
-            stage[lvl][u % 2] = (out + got[pl.ds(go, half)].astype(jnp.float32)).astype(jnp.bfloat16)
+            stage[lvl][u % STAGE_SLOTS] = (out + got[pl.ds(go, half)].astype(jnp.float32)).astype(jnp.bfloat16)
             keep[lvl][u % 2] = mine + got[pl.ds(st, half)].astype(jnp.float32)
             reduce_copy(lvl, u).start()
         else:
@@ -132,27 +130,31 @@
         for j in range(4):
             pl.when(t % PER == 0)(lambda: a_copy(m, block[j]).wait())
             if j == 0:
-                pl.when(t >= 2)(lambda: reduce_copy(0, t - 2).wait_send())
+                pl.when(t >= STAGE_SLOTS)(lambda: reduce_copy(0, t - STAGE_SLOTS).wait_send())
             r = lax.dot_general(a_v[block[j]], g_v[t % 2], (((0,), (0,)), ((), ())),
                                 preferred_element_type=jnp.float32)
             if j < 2:
-                s0[t % 2, j * 256:(j + 1) * 256] = r.astype(jnp.bfloat16)
+                s0[t % STAGE_SLOTS, j * 256:(j + 1) * 256] = r.astype(jnp.bfloat16)
             else:
                 p_v[t % 2, j - 2] = r
             pl.when(t == PER - 1)(lambda: a_copy(1, block[j]).start())
             if j == 1:
                 reduce_copy(0, t).start()
-            for s, lag, gap in REDUCE:
-                if gap == j:
-                    pl.when(t >= lag)(lambda: run(s, t - lag))
-            for s, off, gap in GATHER:
-                if gap == j:
-                    pl.when((t >= off) & ((t - off) % 2 == 0))(lambda: run(s, (t - off) // 2))
+            i = 4 * t + j
+            for s, at_block in enumerate(REDUCE, 1):
+                if at_block % 4 == j:
+                    pl.when(t >= at_block // 4)(lambda: run(s, t - at_block // 4))
+            for s, at_block in enumerate(GATHER, 6):
+                due = i - at_block
+                if RATE != 4:
+                    pl.when((due >= 0) & (lax.rem(due + 8 * RATE * 4, RATE) == 0))(lambda: run(s, due // RATE))
+                elif at_block % 4 == j:
+                    pl.when(t >= at_block // 4)(lambda: run(s, t - at_block // 4))
 
     for s, u in TAIL:
         run(s, u)
     for lvl in range(LEVELS):
-        for u in range(UNITS - 2, UNITS):
+        for u in range(UNITS - STAGE_SLOTS, UNITS):
             reduce_copy(lvl, u).wait_send()
         for u in range(UNITS - SEND_SLOTS, UNITS):
             gather_copy(lvl, u).wait_send()
@@ -171,7 +173,7 @@
                 pltpu.VMEM((2, TOKENS, COLS), bf16),
                 pltpu.VMEM((2, 2, 256, COLS), f32),
                 *(pltpu.VMEM((2, rows, COLS), f32) for rows in ROWS[1:]),
-                *(pltpu.VMEM((2, rows, COLS), bf16) for rows in ROWS),
+                *(pltpu.VMEM((STAGE_SLOTS, rows, COLS), bf16) for rows in ROWS),
                 *(pltpu.VMEM((UNITS, rows, COLS), bf16) for rows in ROWS),
                 pltpu.SemaphoreType.DMA((4,)),
                 pltpu.SemaphoreType.DMA((2,)),

time: 178 us -> 165 us (0.927)
  Pallas kernels: 171 us -> 158 us
    pallas_call x1, Pallas kernels: 171 us -> 158 us  [body(): pl.pallas_call(kernel, out_shape=pltpu.VMEM((MATS, D, FF), bf16), in_spec...]
where the time goes in v2:
time: 165 us; the launch traced here: 164 us
  Pallas kernels  158 us (96%)
  local copies, waits for them, and re-layouts  6.16 us (4%)
    pallas_call x1, Pallas kernels, body(): pl.pallas_call(kernel, out_shape=pltpu.VMEM((MATS, D, FF), bf16), in_spec...  158 us
    unnamed x1, local copies, waits for them, and re-layouts  6.16 us

profile of v2, /device:TPU:0, one launch (start us, length us, event | category | flops | bytes accessed | tf_op | source)
XLA Modules:
  0.0 164.4 jit_solution(12049005729650616077)
XLA Ops:
  0.0 158.2 %sum_units.1 = bf16[2,1024,4096]{2,1,0:T(8,128)(2,1)S(1)} custom-call(bf16[1,2,4096,1024]{3,2,1,0:T(8,128)(2,1)} %a_ref.1, bf16[1,2,4096,4096]{3,2,1,0:T(8,128)(2,1)} %g_ref.1), custom_call_target="tpu_custom_call" | custom-call | flops 68719476736 | bytes 88080384 | tf_op jit(solution)/shard_map/sum_units/pallas_call | solution.py:166
  158.2 6.2 %copy.4 = bf16[2,1024,4096]{2,1,0:T(8,128)(2,1)} copy(bf16[2,1024,4096]{2,1,0:T(8,128)(2,1)S(1)} %sum_units.1) | data formatting | bytes 33554432

commit v3 on v2

--- a/solution.py
+++ b/solution.py
@@ -12,18 +12,17 @@
 UNITS = MATS * PER
 ROWS = (512, 256, 128, 64, 32)
 LEVELS = 5
-STAGE_SLOTS = 2
-SEND_SLOTS = 8
-
-REDUCE = (3, 7, 13, 16, 22)
-GATHER, RATE = (25, 29, 40, 51), 5
+STAGE_SLOTS = 4
+SEND_SLOTS = 16
+
+REDUCE = (3, 7, 13, 17, 21)
+GATHER, RATE = (25, 27, 33, 47), 4
 TAIL = (
-    (3, 13), (10, 0), (6, 8), (10, 1), (8, 5), (9, 3), (6, 9), (7, 7), (10, 2), (9, 4), (10, 3), (8, 6),
-    (4, 12), (10, 4), (5, 11), (6, 10), (2, 15), (4, 13), (3, 14), (7, 8), (8, 7), (9, 5), (7, 9), (5, 12),
-    (10, 5), (6, 11), (9, 6), (3, 15), (7, 10), (4, 14), (10, 6), (5, 13), (8, 8), (9, 7), (7, 11), (4, 15),
-    (10, 7), (8, 9), (6, 12), (9, 8), (8, 10), (10, 8), (5, 14), (9, 9), (6, 13), (7, 12), (10, 9), (8, 11),
-    (9, 10), (5, 15), (7, 13), (6, 14), (10, 10), (8, 12), (9, 11), (6, 15), (7, 14), (10, 11), (8, 13), (9, 12),
-    (7, 15), (8, 14), (10, 12), (9, 13), (10, 13), (8, 15), (9, 14), (10, 14), (9, 15), (10, 15),
+    (4, 12), (3, 13), (10, 0), (10, 1), (10, 2), (9, 5), (10, 3), (9, 6), (8, 8), (5, 11), (10, 4), (9, 7),
+    (6, 10), (10, 5), (10, 6), (3, 14), (10, 7), (2, 15), (4, 13), (8, 9), (9, 8), (5, 12), (7, 10), (6, 11),
+    (4, 14), (10, 8), (3, 15), (9, 9), (5, 13), (7, 11), (6, 12), (4, 15), (10, 9), (8, 10), (5, 14), (7, 12),
+    (6, 13), (8, 11), (9, 10), (5, 15), (7, 13), (6, 14), (10, 10), (8, 12), (9, 11), (6, 15), (7, 14), (10, 11),
+    (8, 13), (9, 12), (7, 15), (10, 12), (8, 14), (9, 13), (10, 13), (8, 15), (9, 14), (10, 14), (9, 15), (10, 15),
 )
 
 
@@ -128,7 +127,12 @@
         g_copy(t).wait()
         m = t // PER
         for j in range(4):
-            pl.when(t % PER == 0)(lambda: a_copy(m, block[j]).wait())
+            if j % 2 == 0:
+                @pl.when(t % PER == 0)
+                def _():
+                    a_copy(m, block[j]).wait()
+                    a_copy(m, block[j + 1]).wait()
+
             if j == 0:
                 pl.when(t >= STAGE_SLOTS)(lambda: reduce_copy(0, t - STAGE_SLOTS).wait_send())
             r = lax.dot_general(a_v[block[j]], g_v[t % 2], (((0,), (0,)), ((), ())),
@@ -137,7 +141,14 @@
                 s0[t % STAGE_SLOTS, j * 256:(j + 1) * 256] = r.astype(jnp.bfloat16)
             else:
                 p_v[t % 2, j - 2] = r
-            pl.when(t == PER - 1)(lambda: a_copy(1, block[j]).start())
+            if j % 2 == 0:
+                continue
+
+            @pl.when(t == PER - 1)
+            def _():
+                a_copy(1, block[j - 1]).start()
+                a_copy(1, block[j]).start()
+
             if j == 1:
                 reduce_copy(0, t).start()
             i = 4 * t + j

time: 165 us -> 161 us (0.976)
  Pallas kernels: 158 us -> 155 us
    pallas_call x1, Pallas kernels: 158 us -> 155 us  [body(): pl.pallas_call(kernel, out_shape=pltpu.VMEM((MATS, D, FF), bf16), in_spec...]
where the time goes in v3:
time: 161 us
  Pallas kernels  155 us (96%)
  local copies, waits for them, and re-layouts  6.16 us (4%)
    pallas_call x1, Pallas kernels, body(): pl.pallas_call(kernel, out_shape=pltpu.VMEM((MATS, D, FF), bf16), in_spec...  155 us
    unnamed x1, local copies, waits for them, and re-layouts  6.16 us

profile of v3, /device:TPU:0, one launch (start us, length us, event | category | flops | bytes accessed | tf_op | source)
XLA Modules:
  0.0 160.7 jit_solution(13717758514706166860)
XLA Ops:
  0.0 154.6 %sum_units.1 = bf16[2,1024,4096]{2,1,0:T(8,128)(2,1)S(1)} custom-call(bf16[1,2,4096,1024]{3,2,1,0:T(8,128)(2,1)} %a_ref.1, bf16[1,2,4096,4096]{3,2,1,0:T(8,128)(2,1)} %g_ref.1), custom_call_target="tpu_custom_call" | custom-call | flops 68719476736 | bytes 88080384 | tf_op jit(solution)/shard_map/sum_units/pallas_call | solution.py:177
  154.6 6.2 %copy.4 = bf16[2,1024,4096]{2,1,0:T(8,128)(2,1)} copy(bf16[2,1024,4096]{2,1,0:T(8,128)(2,1)S(1)} %sum_units.1) | data formatting | bytes 33554432
